TPU v7x, 32 devices: a whole 2x2x4 slice. The times are simulated.
32 devices in a mesh: member: 4 (over y, x), region: 2 (over core), block: 4 (over z).
Axes of the slice: x: 2, y: 2, z: 4, core: 2. Of those that a mesh axis runs over, the one named last changes fastest.
Arguments:
- traffic_load: float32 [128, 65536], P('member', ('region', 'block')), may hold values from 0.05 to 0.7
- free_speed: float32 [65536], P(('region', 'block')), may hold values from 0.3 to 0.95
- wave_speed: float32 [65536], P(('region', 'block')), may hold values from 0.15 to 0.6
- jam_density: float32 [65536], P(('region', 'block')), may hold values from 0.8 to 1.2
- capacity_share: float32 [65536], P(('region', 'block')), may hold values from 0.5 to 1
- observation_cell: int32 [24576], P(('region', 'block')), may hold values from 0 to 2047
- obs_count: int32 [32], P(('region', 'block')), may hold values from 1 to 768, 12288 in all
- observation_value: float32 [24576], P(('region', 'block')), may hold values from 0 to 0.8
- observation_variance: float32 [24576], P(('region', 'block')), may hold values from 0.002 to 0.02
- observation_noise: float32 [128, 24576], P('member', ('region', 'block')), may hold values from -6 to 6
- block_lists: int32 [32, 3], P(('region', 'block')), may hold values from 0 to 31, as said below
Outputs:
- analysis: float32 [128, 65536], P('member', ('region', 'block'))
Inputs may be any that keep to these rules, and one draw needn't show every extreme that they name: `block_lists`: row b lists 3 different blocks, b itself among them, each within 4 blocks of b.
All inputs are finite; a program needn't handle non-finite values. No bound on the sum of `obs_count` on one device may be relied on, other than what follows from the above.
Results may differ from a plain program's by a relative error of at most 0.0003.
Values sent between devices are 32-bit elements; how exact they have to be, the bound alone decides.
A program may use at most 64 MiB of HBM per device.

v0:
```python
import jax
import jax.numpy as jnp
from jax import lax
from jax.sharding import PartitionSpec as P

REALIZATION_TALLY = 128
HORIZON_TICKS = 16
CELLS_PER_BLOCK = 2048
BLOCK_SLOTS = 768


def padded(value, sides, width):
    for axis, dim in sides:
        size, length = (lax.axis_size(axis), value.shape[dim])
        up = [(i, (i + 1) % size) for i in range(size - 1)]
        down = [(j, i) for i, j in up]
        last = lax.slice_in_dim(value, length - width, length, axis=dim)
        leading = lax.slice_in_dim(value, 0, width, axis=dim)
        before = lax.ppermute(last, axis, up)
        after = lax.ppermute(leading, axis, down)
        value = jnp.concatenate([before, value, after], axis=dim)
    return value


def road_capacity(free_speed, wave_speed, jam_density, capacity_share):
    return capacity_share * free_speed * wave_speed * jam_density / (free_speed + wave_speed)


def block_products(left_side, right_side, weight, block_total):
    member_count = left_side.shape[0]
    left_blocks = (left_side * weight).reshape(member_count, block_total, -1)
    right_blocks = right_side.reshape(member_count, block_total, -1)
    return jnp.einsum("kbo,jbo->bkj", left_blocks, right_blocks, precision=lax.Precision.HIGHEST)


def body(
    traffic_load,
    free_speed,
    wave_speed,
    jam_density,
    capacity_share,
    observation_cell,
    obs_count,
    observation_value,
    observation_variance,
    observation_noise,
    block_lists,
):
    mem_local, cell_total = traffic_load.shape
    block_total = obs_count.shape[0]
    slot_total = observation_cell.shape[0]
    capacity = road_capacity(free_speed, wave_speed, jam_density, capacity_share)
    is_last = lax.axis_index(("region", "block")) == lax.axis_size(("region", "block")) - 1
    margin = HORIZON_TICKS
    state_wide = padded(traffic_load, ((("region", "block"), 1),), margin)
    road_wide = padded(
        jnp.stack([free_speed, wave_speed, jam_density, capacity]),
        ((("region", "block"), 1),),
        margin,
    )
    speed_wide = road_wide[0]
    wave_wide = road_wide[1]
    jam_wide = road_wide[2]
    capacity_wide = road_wide[3]
    exit_mask = (jnp.arange(cell_total + 2 * margin) == cell_total + margin) & is_last
    exit_value = capacity[-1]

    def advance_wide(step_index, state):
        demand = jnp.minimum(speed_wide * state, capacity_wide)
        supply = jnp.minimum(capacity_wide, wave_wide * (jam_wide - state))
        supply = jnp.where(exit_mask[None, :], exit_value, supply)
        fluxes = jnp.minimum(demand[:, :-1], supply[:, 1:])
        updated = state[:, 1:-1] + fluxes[:, :-1] - fluxes[:, 1:]
        return state.at[:, 1:-1].set(updated)

    predicted_traffic_load = lax.fori_loop(0, HORIZON_TICKS, advance_wide, state_wide)[
        :, margin : margin + cell_total
    ]
    realization_total = lax.psum(jnp.sum(predicted_traffic_load, axis=0), "member")
    realization_average = realization_total / REALIZATION_TALLY
    realization_departure = predicted_traffic_load - realization_average
    slot_cell_index = (
        jnp.arange(slot_total, dtype=jnp.int32) // BLOCK_SLOTS * CELLS_PER_BLOCK + observation_cell
    )
    obs_anomaly = jnp.take(realization_departure, slot_cell_index, axis=1)
    obs_mean = jnp.take(realization_average, slot_cell_index)
    live_mask = (
        (jnp.arange(BLOCK_SLOTS, dtype=jnp.int32)[None, :] < obs_count[:, None])
        .reshape(-1)
        .astype(jnp.float32)
    )
    weight = live_mask / observation_variance
    misfit = observation_value - obs_mean
    obs_all, noise_all = (
        lax.all_gather(obs_anomaly, "member", axis=0, tiled=True),
        lax.all_gather(observation_noise, "member", axis=0, tiled=True),
    )
    spread = jnp.sum(obs_all * obs_all, axis=0) / (REALIZATION_TALLY - 1)
    misfit_sum, spread_sum = lax.psum(
        (
            jnp.sum(misfit * misfit * weight),
            jnp.sum(live_mask * (spread / observation_variance + 1.0)),
        ),
        ("region", "block"),
    )
    inflation = jnp.sqrt(misfit_sum / spread_sum)
    perturbed = misfit + jnp.sqrt(observation_variance) * noise_all
    scaled = inflation * obs_all
    gram_part = block_products(scaled, scaled, weight, block_total)
    cross_part = block_products(scaled, perturbed - scaled, weight, block_total)
    neighbour_pairs = padded(
        jnp.stack([gram_part, cross_part]), ((("region", "block"), 1),), block_total
    )
    first_block = (lax.axis_index(("region", "block")) - 1) * block_total
    relative = block_lists - first_block
    selector = jnp.sum(
        (
            relative[:, :, None] == jnp.arange(3 * block_total, dtype=jnp.int32)[None, None, :]
        ).astype(jnp.float32),
        axis=1,
    )
    local_gram = jnp.einsum(
        "be,ekj->bkj", selector, neighbour_pairs[0], precision=lax.Precision.HIGHEST
    )
    local_cross = jnp.einsum(
        "be,ekj->bkj", selector, neighbour_pairs[1], precision=lax.Precision.HIGHEST
    )
    identity = (REALIZATION_TALLY - 1) * jnp.eye(REALIZATION_TALLY, dtype=jnp.float32)[None]
    system = identity + local_gram
    factors = jnp.linalg.cholesky(system)
    mixing = jax.vmap(lambda factor, target: jax.scipy.linalg.cho_solve((factor, True), target))(
        factors, local_cross
    )
    member_start = lax.axis_index("member") * mem_local
    own_columns = lax.dynamic_slice_in_dim(mixing, member_start, mem_local, 2)
    row_piece = lax.all_gather(realization_departure, "member", axis=0, tiled=True)
    row_count = row_piece.shape[0]
    piece_blocks = row_piece.reshape(row_count, block_total, CELLS_PER_BLOCK)
    change = (
        jnp.zeros((mem_local, block_total, CELLS_PER_BLOCK), jnp.float32)
        + jnp.einsum("kbc,bkj->jbc", piece_blocks, own_columns, precision=lax.Precision.HIGHEST)
    ).reshape(mem_local, cell_total)
    return realization_average + inflation * realization_departure + inflation * change


def solution(mesh):
    placed = (
        P("member", ("region", "block")),
        P(("region", "block")),
        P(("region", "block")),
        P(("region", "block")),
        P(("region", "block")),
        P(("region", "block")),
        P(("region", "block")),
        P(("region", "block")),
        P(("region", "block")),
        P("member", ("region", "block")),
        P(("region", "block"), None),
    )
    return jax.shard_map(
        body,
        mesh=mesh,
        in_specs=placed,
        out_specs=P("member", ("region", "block")),
        check_vma=False,
    )
```

profile of v0, /device:TPU:0, one launch (start us, length us, event | category | flops | bytes accessed | tf_op | source)
XLA Modules:
  0.0 368.9 jit_solution(8760085229739747867)
XLA Ops:
  8.4 4.9 %collective-permute-start.2 = (f32[4,16]{1,0:T(4,128)S(1)}, f32[4,16]{1,0:T(4,128)S(1)}, u32[]{:S(2)}, u32[]{:S(2)}) collective-permute-start(f32[4,16]{1,0:T(4,128)S(1)} %get-tuple-element.210), channel_id=1, source_target_pairs={{0,1},{1,2},{2,3},{3,4},{4,5},{5,6},{6,7},{8,9},{9,10},{10,11},{11... | collective-permute-start | bytes 776 | tf_op jit(solution)/shard_map/ppermute | solution.py:19
  15.5 4.5 %collective-permute-start = (f32[32,16]{1,0:T(8,128)S(1)}, f32[32,16]{1,0:T(8,128)S(1)}, u32[]{:S(2)}, u32[]{:S(2)}) collective-permute-start(f32[32,16]{1,0:T(8,128)S(1)} %get-tuple-element.204), channel_id=1, source_target_pairs={{0,1},{1,2},{2,3},{3,4},{4,5},{5,6},{6,7},{8,9},{9,10},{10,11},{11... | collective-permute-start | bytes 6152 | tf_op jit(solution)/shard_map/ppermute | solution.py:19
  26.4 90.7 %while.15 = (s32[]{:T(128)}, f32[32,8224]{1,0:T(8,128)S(1)}, pred[]{:T(512)}, f32[1,8224]{1,0:T(1,128)S(1)}, f32[1,8224]{1,0:T(1,128)S(1)}, /*index=5*/f32[]{:T(...) while((s32[]{:T(128)}, f32[32,8224]{1,0:T(8,128)S(1)}, ...), condition=%wide.region_2.3_spmd.clone, body=%wide.region_1.0_spmd.clone.sunk | while | flops 2647714 | bytes 10195928 | solution.py:76
  28.1 1.3 fusion.48
  29.4 2.7 scatter.7
  33.8 1.3 fusion.48
  35.1 2.7 scatter.7
  39.5 1.3 fusion.48
  40.8 2.7 scatter.7
  45.1 1.3 fusion.48
  46.4 2.7 scatter.7
  50.8 1.3 fusion.48
  52.1 2.7 scatter.7
  57.8 2.7 scatter.7
  63.4 2.7 scatter.7
  69.1 2.7 scatter.7
  74.8 2.7 scatter.7
  79.1 1.3 fusion.48
  80.4 2.7 scatter.7
  84.8 1.3 fusion.48
  86.1 2.7 scatter.7
  91.8 2.7 scatter.7
  97.4 2.7 scatter.7
  103.1 2.7 scatter.7
  108.8 2.7 scatter.7
  114.5 2.7 scatter.7
  117.5 16.3 %psum.21 = f32[8192]{0:T(1024)S(1)} all-reduce(f32[8192]{0:T(1024)S(1)} %slice_reduce_fusion), channel_id=1, replica_groups=mesh['member'=4,'region'=2,'block'=4] {'member'}, use_global_device_ids=true, to_apply=%region_4.5 | all-reduce | flops 8192 | bytes 65536 | tf_op jit(solution)/shard_map/psum | solution.py:79
  134.1 2.7 copy.79
  136.8 17.4 %gather_fusion = f32[3072]{0:T(1024)S(1)} fusion(f32[8192]{0:T(1024)S(1)} %broadcast_multiply_fusion.2, s32[3072]{0:T(1024)S(1)} %broadcast_clamp_fusion), kind=kCustom, calls=%fused_computation | custom fusion | bytes 36864 | tf_op jit(solution)/shard_map/jit(_take)/gather | solution.py:86
  154.3 13.0 %gather_fusion.1 = f32[3072,32]{1,0:T(8,128)} fusion(f32[32,8192]{0,1:T(8,128)} %copy.79, s32[3072]{0:T(1024)S(1)} %broadcast_clamp_fusion), kind=kCustom, calls=%fused_computation.1 | custom fusion | bytes 798720 | tf_op jit(solution)/shard_map/jit(_take)/gather | solution.py:85
  168.0 2.7 select_bitcast_fusion
  172.7 3.1 copy.85
  175.8 27.7 %all-gather.4.cloned.1.call-done = f32[128,3072]{1,0:T(8,128)} async-done(((f32[32,3072]{1,0:T(8,128)}), f32[128,3072]{1,0:T(8,128)}) %all-gather.4.cloned.1.call-update) | async-done | bytes 1572880 | tf_op jit(solution)/shard_map/all_gather | solution.py:95
  203.5 1.7 multiply_reduce_fusion
  205.9 17.1 %all-reduce = (f32[]{:T(128)}, f32[]{:T(128)}) all-reduce(f32[]{:T(128)} %get-tuple-element.195, f32[]{:T(128)} %select_reduce_fusion.1), channel_id=1, replica_groups=mesh['member'=4,'region'=2,'block'=4] {'region','block'}, use_global_device_ids=true, to_apply=%region_6.7 | all-reduce | flops 2 | bytes 16 | tf_op jit(solution)/shard_map/psum | solution.py:99
  224.3 1.6 copy.82
  226.0 3.2 add_subtract_fusion
  229.6 2.7 convolution_bitcast_fusion.1
  232.4 2.7 convolution_bitcast_fusion
  235.1 1.7 collective-permute-start.4
  236.8 1.5 collective-permute-start.5
  238.6 10.0 %collective-permute-done.4 = f32[2,4,128,128]{3,2,1,0:T(8,128)S(1)} collective-permute-done((f32[2,4,128,128]{3,2,1,0:T(8,128)S(1)}, f32[2,4,128,128]{3,2,1,0:T(8,128)S(1)}, u32[]{:S(2)}, u32[]{:S(2)}) %collective-permute-start.4) | collective-permute-done | bytes 524320 | tf_op jit(solution)/shard_map/ppermute | solution.py:19
  248.6 10.3 %collective-permute-done.5 = f32[2,4,128,128]{3,2,1,0:T(8,128)S(1)} collective-permute-done((f32[2,4,128,128]{3,2,1,0:T(8,128)S(1)}, f32[2,4,128,128]{3,2,1,0:T(8,128)S(1)}, u32[]{:S(2)}, u32[]{:S(2)}) %collective-permute-start.5) | collective-permute-done | bytes 524320 | tf_op jit(solution)/shard_map/ppermute | solution.py:20
  260.5 46.9 %custom-call.11 = f32[4,128,128]{2,1,0:T(8,128)S(1)} custom-call(f32[4,128,128]{2,1,0:T(8,128)S(1)} %fusion.19), custom_call_target="Cholesky" | custom-call | tf_op jit(solution)/shard_map/jit(cholesky)/cholesky | solution.py:130
  307.7 39.3 %custom-call.12 = f32[4,1,128,128]{2,3,1,0:T(8,128)S(1)} custom-call(f32[4,1,128,128]{3,2,1,0:T(8,128)S(1)} %select_bitcast_fusion.1), custom_call_target="InvertDiagBlocksLowerTriangular" | custom-call | tf_op jit(solution)/shard_map/vmap(jit(_cho_solve))/triangular_solve | solution.py:131
  349.4 5.6 %copy.96 = f32[128,8192]{0,1:T(8,128)} copy(f32[128,8192]{1,0:T(8,128)} %all-gather.8.cloned.1.call-done) | data formatting | bytes 8388608 | tf_op jit(solution)/shard_map/all_gather | solution.py:136
  355.0 6.0 %fusion.9 = f32[4,4,8,2048]{3,2,1,0:T(8,128)S(1)} fusion(f32[128,4,2048]{0,2,1:T(8,128)} %bitcast.50, f32[]{:T(128)S(6)} %sqrt.6, f32[4,128,128]{1,2,0:T(8,128)S(1)} %fusion.14, s32[]{:T(128)S(6)} %select_n.38), kind=kOutput, calls=%fused_computation.16 | convolution fusion | flops 402915328 | bytes 5308424 | tf_op jit(solution)/shard_map/kbc,bkj->jbc/dot_general | solution.py:141
  361.0 1.3 add_add_fusion
  (235 shorter events, 57.3 us)
Async XLA Ops:
  6.5 19.2 %copy-start.2 = (f32[32,8192]{1,0:T(8,128)S(1)}, f32[32,8192]{1,0:T(8,128)}, u32[]{:S(2)}) copy-start(f32[32,8192]{1,0:T(8,128)} %param.15) | copy-start | bytes 3145732
  6.5 166.2 %all-gather.6.cloned.1.call-start = ((), (), s32[]{:S(2)}) async-start(), calls=%async_computation.1 | async-start | bytes 1966080 | tf_op jit(solution)/shard_map/all_gather | solution.py:96
  8.4 15.8 %collective-permute-start.2 = (f32[4,16]{1,0:T(4,128)S(1)}, f32[4,16]{1,0:T(4,128)S(1)}, u32[]{:S(2)}, u32[]{:S(2)}) collective-permute-start(f32[4,16]{1,0:T(4,128)S(1)} %get-tuple-element.210), channel_id=1, source_target_pairs={{0,1},{1,2},{2,3},{3,4},{4,5},{5,6},{6,7},{8,9},{9,10},{10,11},{11... | collective-permute-start | bytes 776 | tf_op jit(solution)/shard_map/ppermute | solution.py:19
  13.4 10.8 %collective-permute-start.3 = (f32[4,16]{1,0:T(4,128)S(1)}, f32[4,16]{1,0:T(4,128)S(1)}, u32[]{:S(2)}, u32[]{:S(2)}) collective-permute-start(f32[4,16]{1,0:T(4,128)S(1)} %get-tuple-element.209), channel_id=1, source_target_pairs={{1,0},{2,1},{3,2},{4,3},{5,4},{6,5},{7,6},{9,8},{10,9},{11,10},{12... | collective-permute-start | bytes 776 | tf_op jit(solution)/shard_map/ppermute | solution.py:20
  15.5 9.0 %collective-permute-start = (f32[32,16]{1,0:T(8,128)S(1)}, f32[32,16]{1,0:T(8,128)S(1)}, u32[]{:S(2)}, u32[]{:S(2)}) collective-permute-start(f32[32,16]{1,0:T(8,128)S(1)} %get-tuple-element.204), channel_id=1, source_target_pairs={{0,1},{1,2},{2,3},{3,4},{4,5},{5,6},{6,7},{8,9},{9,10},{10,11},{11... | collective-permute-start | bytes 6152 | tf_op jit(solution)/shard_map/ppermute | solution.py:19
  20.1 5.6 %collective-permute-start.1 = (f32[32,16]{1,0:T(8,128)S(1)}, f32[32,16]{1,0:T(8,128)S(1)}, u32[]{:S(2)}, u32[]{:S(2)}) collective-permute-start(f32[32,16]{1,0:T(8,128)S(1)} %get-tuple-element.203), channel_id=1, source_target_pairs={{1,0},{2,1},{3,2},{4,3},{5,4},{6,5},{7,6},{9,8},{10,9},{11,10},{12... | collective-permute-start | bytes 6152 | tf_op jit(solution)/shard_map/ppermute | solution.py:20
  21.4 182.1 %all-gather.4.cloned.1.call-start = ((), (), s32[]{:S(2)}) async-start(), calls=%async_computation | async-start | bytes 1966080 | tf_op jit(solution)/shard_map/all_gather | solution.py:95
  134.1 2.7 copy-start
  154.2 13.0 %copy-start.3 = (f32[3072]{0:T(1024)S(1)}, f32[3072]{0:T(1024)}, u32[]{:S(2)}) copy-start(f32[3072]{0:T(1024)} %param.23) | copy-start | bytes 36868
  154.3 13.0 %copy-start.4 = (s32[3072]{0:T(1024)S(1)}, s32[3072]{0:T(1024)}, u32[]{:S(2)}) copy-start(s32[3072]{0:T(1024)} %param.20) | copy-start | bytes 36868
  154.3 13.0 %copy-start.5 = (f32[3072]{0:T(1024)S(1)}, f32[3072]{0:T(1024)}, u32[]{:S(2)}) copy-start(f32[3072]{0:T(1024)} %param.22) | copy-start | bytes 36868
  172.0 177.4 %all-gather.8.cloned.1.call-start = ((), (), s32[]{:S(2)}) async-start(), calls=%async_computation.2 | async-start | bytes 5242880 | tf_op jit(solution)/shard_map/all_gather | solution.py:136
  203.5 20.8 %copy-start.1 = (f32[128,3072]{1,0:T(8,128)S(1)}, f32[128,3072]{1,0:T(8,128)}, u32[]{:S(2)}) copy-start(f32[128,3072]{1,0:T(8,128)} %all-gather.4.cloned.1.call-done) | copy-start | bytes 4718596
  232.3 6.0 %copy-start.6 = (s32[4,3]{1,0:T(4,128)S(1)}, s32[4,3]{1,0:T(4,128)}, u32[]{:S(2)}) copy-start(s32[4,3]{1,0:T(4,128)} %param.25) | copy-start | bytes 148
  235.1 13.5 %collective-permute-start.4 = (f32[2,4,128,128]{3,2,1,0:T(8,128)S(1)}, f32[2,4,128,128]{3,2,1,0:T(8,128)S(1)}, u32[]{:S(2)}, u32[]{:S(2)}) collective-permute-start(f32[2,4,128,128]{3,2,1,0:T(8,128)S(1)} %pad_maximum_fusion.1), channel_id=1, source_target_pairs={{0,1},{1,2},{2,3},{3,4},{4,5},{5,6},{6,7},{8,9},{9,10},{10,11},{11... | collective-permute-start | bytes 1572872 | tf_op jit(solution)/shard_map/ppermute | solution.py:19
  236.8 22.2 %collective-permute-start.5 = (f32[2,4,128,128]{3,2,1,0:T(8,128)S(1)}, f32[2,4,128,128]{3,2,1,0:T(8,128)S(1)}, u32[]{:S(2)}, u32[]{:S(2)}) collective-permute-start(f32[2,4,128,128]{3,2,1,0:T(8,128)S(1)} %pad_maximum_fusion.1), channel_id=1, source_target_pairs={{1,0},{2,1},{3,2},{4,3},{5,4},{6,5},{7,6},{9,8},{10,9},{11,10},{12... | collective-permute-start | bytes 1572872 | tf_op jit(solution)/shard_map/ppermute | solution.py:20
Sparse Core Ops, SparseCore 0:
  21.5 33.1 all-gather.5
  172.1 31.4 all-gather.3
  205.4 52.5 all-gather.7
where the time goes:
time: 370 us; the launch traced here: 369 us
  other arithmetic  144 us (39%)
  local copies, waits for them, and re-layouts  95.2 us (26%)
  waiting for transfers between devices  50 us (14%)
  blocking collectives  33.4 us (9%)
  starting transfers between devices  15.3 us (4%)
  matrix products  14.8 us (4%)
  between operations  14.8 us (4%)
    another operation x4, other arithmetic, body(): factors = jnp.linalg.cholesky(system)  47.1 us
    scatter x16, local copies, waits for them, and re-layouts, advance_wide(): return state.at[:, 1:-1].set(updated)  42.5 us
    another operation x3, other arithmetic, body(): jax.scipy.linalg.cho_solve((factor, True), target)  39.4 us
    all_gather x1, waiting for transfers between devices, body(): lax.all_gather(obs_anomaly, 'member', axis=0, tiled=True)  27.7 us
    another operation x17, other arithmetic  21.6 us
    gather x1, local copies, waits for them, and re-layouts, body(): obs_mean = jnp.take(realization_average, slot_cell_index)  17.4 us
    psum x1, blocking collectives, body(): lax.psum((jnp.sum(misfit * misfit * weight), jnp.sum(live_mask * (spread...  17.1 us
    psum x1, blocking collectives, body(): lax.psum(jnp.sum(predicted_traffic_load, axis=0), 'member')  16.3 us
  transfers between devices with their start and end apart: 9, of which 4 were waited for; matrix products, arithmetic and copies ran while one was open for 65% of the time, Pallas kernels for 0%

commit v1 on v0

v1 whole, which is shorter than its diff:
```python
import functools

import jax
import jax.numpy as jnp
from jax import lax
from jax.experimental import pallas as pl
from jax.experimental.pallas import tpu as pltpu
from jax.sharding import PartitionSpec as P

HORIZON_TICKS = 16
HALO = 128
HIGHEST = lax.Precision.HIGHEST
MESH = pl.DeviceIdType.MESH
VMEM = pl.BlockSpec(memory_space=pltpu.VMEM)
SMEM = pl.BlockSpec(memory_space=pltpu.SMEM)


def position(regions, blocks):
    slab = lax.axis_index("region") * blocks + lax.axis_index("block")
    return lax.axis_index("member"), slab


def device(member, slab, blocks):
    return {"member": member, "region": lax.div(slab, blocks), "block": lax.rem(slab, blocks)}


def remote(src, dst, send_sem, recv_sem, target):
    return pltpu.make_async_remote_copy(
        src_ref=src,
        dst_ref=dst,
        send_sem=send_sem,
        recv_sem=recv_sem,
        device_id=target,
        device_id_type=MESH,
    )


def greet(target):
    pl.semaphore_signal(
        pltpu.get_barrier_semaphore(), inc=1, device_id=target, device_id_type=MESH
    )


def scatter_kernel(
    sizes,
    load,
    noise,
    road,
    state,
    noise_all,
    road_all,
    main_send,
    main_recv,
    left_send,
    left_recv,
    right_send,
    right_recv,
    noise_send,
    noise_recv,
    edge_send,
    road_send,
    road_recv,
):
    members, regions, blocks = sizes
    slabs = regions * blocks
    me, slab = position(regions, blocks)
    rows = load.shape[0]
    cells = load.shape[1] // members
    slots = noise.shape[1] // members
    has_left, has_right = slab > 0, slab < slabs - 1
    first, last = me == 0, me == members - 1

    for r in range(1, members):
        greet(device(lax.rem(me + r, members), slab, blocks))

    @pl.when(first & has_left)
    def _():
        for other in range(members):
            greet(device(other, slab - 1, blocks))

    @pl.when(last & has_right)
    def _():
        for other in range(members):
            greet(device(other, slab + 1, blocks))

    pl.semaphore_wait(
        pltpu.get_barrier_semaphore(),
        members - 1 + has_left.astype(jnp.int32) + has_right.astype(jnp.int32),
    )

    mine = pl.ds(pl.multiple_of(me * rows, rows), rows)
    centre = pl.ds(HALO, cells)
    left = pl.ds(0, HALO)
    right = pl.ds(HALO + cells, HALO)

    def own(start, size):
        return pl.ds(pl.multiple_of(start, HALO), size)

    def edge_right():
        return remote(
            load.at[:, members * cells - HALO :],
            state.at[mine, left],
            edge_send.at[0],
            left_recv.at[me],
            device(0, slab + 1, blocks),
        )

    def edge_left():
        return remote(
            load.at[:, :HALO],
            state.at[mine, right],
            edge_send.at[1],
            right_recv.at[me],
            device(members - 1, slab - 1, blocks),
        )

    def road_right():
        return remote(
            road.at[:, members * cells - HALO :],
            road_all.at[:, left],
            road_send.at[0],
            road_recv.at[0],
            device(0, slab + 1, blocks),
        )

    def road_left():
        return remote(
            road.at[:, :HALO],
            road_all.at[:, right],
            road_send.at[1],
            road_recv.at[1],
            device(members - 1, slab - 1, blocks),
        )

    def main_copy(r):
        to = lax.rem(me + r, members)
        return remote(
            load.at[:, own(to * cells, cells)],
            state.at[mine, centre],
            main_send.at[r - 1],
            main_recv.at[me],
            device(to, slab, blocks),
        )

    def left_copy(r):
        to = lax.rem(me + r, members)
        return to > 0, remote(
            load.at[:, own(jnp.maximum(to * cells - HALO, 0), HALO)],
            state.at[mine, left],
            left_send.at[r - 1],
            left_recv.at[me],
            device(to, slab, blocks),
        )

    def right_copy(r):
        to = lax.rem(me + r, members)
        return to < members - 1, remote(
            load.at[:, own(jnp.minimum((to + 1) * cells, (members - 1) * cells), HALO)],
            state.at[mine, right],
            right_send.at[r - 1],
            right_recv.at[me],
            device(to, slab, blocks),
        )

    def noise_copy(r):
        to = lax.rem(me + r, members)
        return remote(
            noise.at[:, own(to * slots, slots)],
            noise_all.at[mine, :],
            noise_send.at[r - 1],
            noise_recv.at[me],
            device(to, slab, blocks),
        )

    @pl.when(has_right)
    def _():
        edge_right().start()

    @pl.when(has_left)
    def _():
        edge_left().start()

    @pl.when(has_right & first)
    def _():
        road_right().start()

    @pl.when(has_left & last)
    def _():
        road_left().start()

    for r in range(1, members):
        for needed, copy in (left_copy(r), right_copy(r)):
            pl.when(needed)(copy.start)
    for r in range(1, members):
        main_copy(r).start()
    for r in range(1, members):
        noise_copy(r).start()

    state[mine, centre] = load[:, own(me * cells, cells)]
    noise_all[mine, :] = noise[:, own(me * slots, slots)]
    road_all[:, centre] = road[:, own(me * cells, cells)]

    @pl.when(jnp.logical_not(first))
    def _():
        spot = own(jnp.maximum(me * cells - HALO, 0), HALO)
        state[mine, left] = load[:, spot]
        road_all[:, left] = road[:, spot]

    @pl.when(jnp.logical_not(last))
    def _():
        spot = own(jnp.minimum((me + 1) * cells, (members - 1) * cells), HALO)
        state[mine, right] = load[:, spot]
        road_all[:, right] = road[:, spot]

    @pl.when(first & jnp.logical_not(has_left))
    def _():
        state[:, left] = jnp.zeros((members * rows, HALO), jnp.float32)
        road_all[:, left] = jnp.zeros((8, HALO), jnp.float32)

    @pl.when(last & jnp.logical_not(has_right))
    def _():
        state[:, right] = jnp.zeros((members * rows, HALO), jnp.float32)
        row = lax.broadcasted_iota(jnp.int32, (8, HALO), 0)
        exit_value = road[:, members * cells - 1 :]
        ghost = jnp.where(row == 1, 1.0, jnp.where(row == 2, 1e30, 0.0))
        road_all[:, right] = jnp.where(row == 3, exit_value, ghost)

    def arrive(dst, sem):
        remote(dst, dst, main_send.at[0], sem, device(lax.rem(me + 1, members), slab, blocks)).wait_recv()

    for r in range(1, members):
        origin = lax.rem(me + r, members)
        from_rows = pl.ds(pl.multiple_of(origin * rows, rows), rows)
        arrive(state.at[from_rows, centre], main_recv.at[origin])
        arrive(noise_all.at[from_rows, :], noise_recv.at[origin])

        @pl.when(jnp.logical_not(first))
        def _():
            arrive(state.at[from_rows, left], left_recv.at[origin])

        @pl.when(jnp.logical_not(last))
        def _():
            arrive(state.at[from_rows, right], right_recv.at[origin])

    @pl.when(first & has_left)
    def _():
        for origin in range(members):
            arrive(state.at[pl.ds(origin * rows, rows), left], left_recv.at[origin])
        arrive(road_all.at[:, left], road_recv.at[0])

    @pl.when(last & has_right)
    def _():
        for origin in range(members):
            arrive(state.at[pl.ds(origin * rows, rows), right], right_recv.at[origin])
        arrive(road_all.at[:, right], road_recv.at[1])

    for r in range(1, members):
        main_copy(r).wait_send()
        noise_copy(r).wait_send()
        for needed, copy in (left_copy(r), right_copy(r)):
            pl.when(needed)(copy.wait_send)

    @pl.when(has_right)
    def _():
        edge_right().wait_send()

    @pl.when(has_left)
    def _():
        edge_left().wait_send()

    @pl.when(has_right & first)
    def _():
        road_right().wait_send()

    @pl.when(has_left & last)
    def _():
        road_left().wait_send()


def block_kernel(
    sizes, counts, state, noise, road, cell, value, variance, anomaly, mean, products, parts, roads, forecast
):
    members, regions, blocks = sizes
    me = lax.axis_index("member")
    rows, width = state.shape
    cells = width - 2 * HALO
    slots = noise.shape[1]
    for i in range(4):
        roads[i] = jnp.broadcast_to(road[i : i + 1, :], (8, width))

    step_rows = 8

    def group(g, total):
        here = pl.ds(pl.multiple_of(g * step_rows, step_rows), step_rows)

        def tick(_, now):
            cap = roads[3]
            demand = jnp.minimum(roads[0] * now, cap)
            supply = jnp.minimum(cap, roads[1] * (roads[2] - now))
            flux = jnp.minimum(demand, pltpu.roll(supply, width - 1, 1))
            return now + pltpu.roll(flux, 1, 1) - flux

        done = lax.fori_loop(0, HORIZON_TICKS, tick, state[here, :])
        inner = done[:, HALO : HALO + cells]
        forecast[here, :] = inner
        return total + inner

    total = lax.fori_loop(0, rows // step_rows, group, jnp.zeros((step_rows, cells), jnp.float32))
    average = jnp.sum(total, axis=0, keepdims=True) / rows
    mean[...] = jnp.broadcast_to(average, mean.shape)

    mine = pl.ds(pl.multiple_of(me * slots, HALO), slots)
    spots = cell[:, mine]
    depth = 256
    picked = jnp.zeros((3 * rows, slots), jnp.float32)
    for c in range(cells // depth):
        part = forecast[:, c * depth : (c + 1) * depth]
        high = part.astype(jnp.bfloat16)
        rest = part - high.astype(jnp.float32)
        middle = rest.astype(jnp.bfloat16)
        low = (rest - middle.astype(jnp.float32)).astype(jnp.bfloat16)
        hot = lax.broadcasted_iota(jnp.int32, (depth, slots), 0) + c * depth == spots
        picked = picked + jnp.dot(
            jnp.concatenate([high, middle, low], axis=0),
            jnp.where(hot, 1.0, 0.0).astype(jnp.bfloat16),
            preferred_element_type=jnp.float32,
        )
        anomaly[:, c * depth : (c + 1) * depth] = part - average[:, c * depth : (c + 1) * depth]
    seen = picked[:rows] + picked[rows : 2 * rows] + picked[2 * rows :]
    obs_mean = jnp.sum(seen, axis=0, keepdims=True) / rows
    departure = seen - obs_mean
    var = variance[:, mine]
    live = (lax.broadcasted_iota(jnp.int32, (1, slots), 1) < counts[me]).astype(jnp.float32)
    weight = live / var
    misfit = value[:, mine] - obs_mean
    spread = jnp.sum(departure * departure, axis=0, keepdims=True) / (rows - 1)
    first = jnp.sum(misfit * misfit * weight, axis=1, keepdims=True)
    second = jnp.sum(live * (spread / var + 1.0), axis=1, keepdims=True)
    row = lax.broadcasted_iota(jnp.int32, parts.shape, 0)
    parts[...] = jnp.where(row == 0, first, jnp.where(row == 1, second, 0.0))
    scaled = departure * weight
    perturbed = misfit + jnp.sqrt(var) * noise[...]
    contract = (((1,), (1,)), ((), ()))
    products[:, :rows] = lax.dot_general(
        scaled, departure, contract, precision=HIGHEST, preferred_element_type=jnp.float32
    )
    products[:, rows:] = lax.dot_general(
        scaled, perturbed, contract, precision=HIGHEST, preferred_element_type=jnp.float32
    )


def neighbour_kernel(
    sizes,
    select,
    products,
    parts,
    total,
    sums,
    slab_in,
    outgoing,
    incoming,
    parts_in,
    parts_sum,
    parts_all,
    slab_send,
    slab_recv,
    plane_send,
    plane_recv,
    part_send,
    part_recv,
    wide_send,
    wide_recv,
):
    members, regions, blocks = sizes
    slabs = regions * blocks
    me, slab = position(regions, blocks)
    has_left, has_right = slab > 0, slab < slabs - 1
    for r in range(1, members):
        greet(device(lax.rem(me + r, members), slab, blocks))
    for r in range(1, slabs):
        greet(device(me, lax.rem(slab + r, slabs), blocks))
    pl.semaphore_wait(pltpu.get_barrier_semaphore(), members + slabs - 2)

    def up():
        return remote(
            products, slab_in.at[0], slab_send.at[0], slab_recv.at[0], device(me, slab + 1, blocks)
        )

    def down():
        return remote(
            products, slab_in.at[1], slab_send.at[1], slab_recv.at[1], device(me, slab - 1, blocks)
        )

    def part_copy(r):
        to = lax.rem(me + r, members)
        return remote(
            parts, parts_in.at[me], part_send.at[r - 1], part_recv.at[me], device(to, slab, blocks)
        )

    def wide_copy(r):
        to = lax.rem(slab + r, slabs)
        return remote(
            parts_sum, parts_all.at[slab], wide_send.at[r - 1], wide_recv.at[slab], device(me, to, blocks)
        )

    def plane_copy(r):
        to = lax.rem(me + r, members)
        return remote(
            outgoing.at[r - 1],
            incoming.at[r - 1],
            plane_send.at[r - 1],
            plane_recv.at[r - 1],
            device(to, slab, blocks),
        )

    for r in range(1, members):
        part_copy(r).start()

    @pl.when(has_right)
    def _():
        up().start()

    @pl.when(has_left)
    def _():
        down().start()

    gathered = parts[...]
    for r in range(1, members):
        origin = lax.rem(me + r, members)
        remote(
            parts, parts_in.at[origin], part_send.at[0], part_recv.at[origin], device(origin, slab, blocks)
        ).wait_recv()
        gathered = gathered + parts_in[origin]
    parts_sum[...] = gathered
    for r in range(1, slabs):
        wide_copy(r).start()

    @pl.when(has_left)
    def _():
        up().wait_recv()

    @pl.when(jnp.logical_not(has_left))
    def _():
        slab_in[0] = jnp.zeros_like(slab_in[0])

    @pl.when(has_right)
    def _():
        down().wait_recv()

    @pl.when(jnp.logical_not(has_right))
    def _():
        slab_in[1] = jnp.zeros_like(slab_in[1])

    def blend(to):
        return (
            select[to * 3] * slab_in[0]
            + select[to * 3 + 1] * products[...]
            + select[to * 3 + 2] * slab_in[1]
        )

    for r in range(1, members):
        outgoing[r - 1] = blend(lax.rem(me + r, members))
        plane_copy(r).start()
    local = blend(me)

    for r in range(1, slabs):
        origin = lax.rem(slab + r, slabs)
        remote(
            parts_sum, parts_all.at[origin], wide_send.at[0], wide_recv.at[origin], device(me, origin, blocks)
        ).wait_recv()
        gathered = gathered + parts_all[origin]
    sums[...] = gathered

    for r in range(1, members):
        plane_copy(r).wait_recv()
        local = local + incoming[r - 1]
    total[...] = local

    for r in range(1, members):
        part_copy(r).wait_send()
        plane_copy(r).wait_send()
    for r in range(1, slabs):
        wide_copy(r).wait_send()

    @pl.when(has_right)
    def _():
        up().wait_send()

    @pl.when(has_left)
    def _():
        down().wait_send()


def dot(a, b):
    return jnp.dot(a, b, precision=HIGHEST, preferred_element_type=jnp.float32)


def invert(block):
    size = block.shape[0]
    row = lax.broadcasted_iota(jnp.int32, (size, size), 0)
    column = lax.broadcasted_iota(jnp.int32, (size, size), 1)
    work = block
    for k in range(size):
        scale = 1.0 / work[k : k + 1, k : k + 1]
        pivot = jnp.where(column[k : k + 1] == k, 1.0, work[k : k + 1, :]) * scale
        factor = work[:, k : k + 1]
        work = jnp.where(
            row == k, pivot, jnp.where(column == k, 0.0, work) - factor * pivot
        )
    return work


def solve_kernel(sizes, total, sums, anomaly, mean, result, work):
    rows = total.shape[0]
    size = 16
    inflation = jnp.sqrt(sums[0:1, 0:1] / sums[1:2, 0:1])
    diagonal = (
        lax.broadcasted_iota(jnp.int32, (rows, rows), 0)
        == lax.broadcasted_iota(jnp.int32, (rows, rows), 1)
    )
    identity = jnp.where(diagonal, float(rows - 1), 0.0)
    work[:, :rows] = identity + inflation * inflation * total[:, :rows]
    work[:, rows:] = identity + inflation * total[:, rows:]
    for p in range(rows // size):
        top, end = p * size, (p + 1) * size
        panel = work[top:end, :]
        update = dot(invert(panel[:, top:end]), panel)
        factor = work[:, top:end]
        work[...] = work[...] - dot(factor, update)
        work[top:end, :] = update
    mixing = inflation * work[:, rows:]
    result[...] = mean[0:1, :] + lax.dot_general(
        mixing,
        anomaly[...],
        (((0,), (0,)), ((), ())),
        precision=HIGHEST,
        preferred_element_type=jnp.float32,
    )


def return_kernel(sizes, result, analysis, send, recv):
    members, regions, blocks = sizes
    me, slab = position(regions, blocks)
    rows = analysis.shape[0]
    cells = result.shape[1]
    for r in range(1, members):
        greet(device(lax.rem(me + r, members), slab, blocks))
    pl.semaphore_wait(pltpu.get_barrier_semaphore(), members - 1)

    def copy(r):
        to = lax.rem(me + r, members)
        return remote(
            result.at[pl.ds(pl.multiple_of(to * rows, rows), rows), :],
            analysis.at[:, pl.ds(pl.multiple_of(me * cells, HALO), cells)],
            send.at[r - 1],
            recv.at[me],
            device(to, slab, blocks),
        )

    for r in range(1, members):
        copy(r).start()
    analysis[:, pl.ds(pl.multiple_of(me * cells, HALO), cells)] = result[
        pl.ds(pl.multiple_of(me * rows, rows), rows), :
    ]
    for r in range(1, members):
        origin = lax.rem(me + r, members)
        spot = analysis.at[:, pl.ds(pl.multiple_of(origin * cells, HALO), cells)]
        remote(spot, spot, send.at[0], recv.at[origin], device(origin, slab, blocks)).wait_recv()
    for r in range(1, members):
        copy(r).wait_send()


def body(
    sizes,
    traffic_load,
    free_speed,
    wave_speed,
    jam_density,
    capacity_share,
    observation_cell,
    obs_count,
    observation_value,
    observation_variance,
    observation_noise,
    block_lists,
):
    members, regions, blocks = sizes
    slabs = regions * blocks
    mem_local, cell_total = traffic_load.shape
    slot_total = observation_cell.shape[0]
    block_total = obs_count.shape[0]
    assert block_total == members
    rows, cells, slots = mem_local * members, cell_total // members, slot_total // members
    f32 = jnp.float32
    dma = pltpu.SemaphoreType.DMA

    capacity = capacity_share * free_speed * wave_speed * jam_density / (free_speed + wave_speed)
    blank = jnp.zeros_like(capacity)
    road = jnp.stack([free_speed, wave_speed, jam_density, capacity, blank, blank, blank, blank])

    state, noise_all, road_all = pl.pallas_call(
        functools.partial(scatter_kernel, sizes),
        out_shape=(
            jax.ShapeDtypeStruct((rows, cells + 2 * HALO), f32),
            jax.ShapeDtypeStruct((rows, slots), f32),
            jax.ShapeDtypeStruct((8, cells + 2 * HALO), f32),
        ),
        in_specs=[VMEM] * 3,
        out_specs=(VMEM,) * 3,
        scratch_shapes=[
            dma((members - 1,)),
            dma((members,)),
            dma((members - 1,)),
            dma((members,)),
            dma((members - 1,)),
            dma((members,)),
            dma((members - 1,)),
            dma((members,)),
            dma((2,)),
            dma((2,)),
            dma((2,)),
        ],
        compiler_params=pltpu.CompilerParams(collective_id=0, has_side_effects=True),
        name="scatter",
    )(traffic_load, observation_noise, road)

    anomaly, mean, products, parts = pl.pallas_call(
        functools.partial(block_kernel, sizes),
        out_shape=(
            jax.ShapeDtypeStruct((rows, cells), f32),
            jax.ShapeDtypeStruct((8, cells), f32),
            jax.ShapeDtypeStruct((rows, 2 * rows), f32),
            jax.ShapeDtypeStruct((8, HALO), f32),
        ),
        in_specs=[SMEM] + [VMEM] * 6,
        out_specs=(VMEM,) * 4,
        scratch_shapes=[
            pltpu.VMEM((4, 8, cells + 2 * HALO), f32),
            pltpu.VMEM((rows, cells), f32),
        ],
        name="block",
    )(
        obs_count,
        state,
        noise_all,
        road_all,
        observation_cell.reshape(1, -1),
        observation_value.reshape(1, -1),
        observation_variance.reshape(1, -1),
    )

    slab = lax.axis_index(("region", "block"))
    named = (slab + jnp.arange(-1, 2, dtype=jnp.int32)) * block_total + lax.axis_index("member")
    select = jnp.sum((block_lists[:, None, :] == named[None, :, None]).astype(f32), axis=2).reshape(-1)

    total, sums = pl.pallas_call(
        functools.partial(neighbour_kernel, sizes),
        out_shape=(
            jax.ShapeDtypeStruct((rows, 2 * rows), f32),
            jax.ShapeDtypeStruct((8, HALO), f32),
        ),
        in_specs=[SMEM, VMEM, VMEM],
        out_specs=(VMEM, VMEM),
        scratch_shapes=[
            pltpu.VMEM((2, rows, 2 * rows), f32),
            pltpu.VMEM((members - 1, rows, 2 * rows), f32),
            pltpu.VMEM((members - 1, rows, 2 * rows), f32),
            pltpu.VMEM((members, 8, HALO), f32),
            pltpu.VMEM((8, HALO), f32),
            pltpu.VMEM((slabs, 8, HALO), f32),
            dma((2,)),
            dma((2,)),
            dma((members - 1,)),
            dma((members - 1,)),
            dma((members - 1,)),
            dma((members,)),
            dma((slabs - 1,)),
            dma((slabs,)),
        ],
        compiler_params=pltpu.CompilerParams(collective_id=1, has_side_effects=True),
        name="neighbours",
    )(select, products, parts)

    result = pl.pallas_call(
        functools.partial(solve_kernel, sizes),
        out_shape=jax.ShapeDtypeStruct((rows, cells), f32),
        in_specs=[VMEM] * 4,
        out_specs=VMEM,
        scratch_shapes=[pltpu.VMEM((rows, 2 * rows), f32)],
        name="solve",
    )(total, sums, anomaly, mean)

    return pl.pallas_call(
        functools.partial(return_kernel, sizes),
        out_shape=jax.ShapeDtypeStruct((mem_local, cell_total), f32),
        in_specs=[VMEM],
        out_specs=VMEM,
        scratch_shapes=[dma((members - 1,)), dma((members,))],
        compiler_params=pltpu.CompilerParams(collective_id=2, has_side_effects=True),
        name="give_back",
    )(result)


def solution(mesh):
    slab = P(("region", "block"))
    placed = (
        P("member", ("region", "block")),
        slab,
        slab,
        slab,
        slab,
        slab,
        slab,
        slab,
        slab,
        P("member", ("region", "block")),
        P(("region", "block"), None),
    )
    sizes = (mesh.shape["member"], mesh.shape["region"], mesh.shape["block"])
    return jax.shard_map(
        functools.partial(body, sizes),
        mesh=mesh,
        in_specs=placed,
        out_specs=P("member", ("region", "block")),
        check_vma=False,
    )
```

time: 370 us -> 130 us (0.35)
  other arithmetic: 144 us -> 0.98 us
  Pallas kernels: 0 us -> 124 us
  local copies, waits for them, and re-layouts: 95.2 us -> 4.67 us
  waiting for transfers between devices: 50 us -> 0 us
  blocking collectives: 33.4 us -> 0 us
  starting transfers between devices: 15.3 us -> 0 us
  matrix products: 14.8 us -> 0 us
  between operations: 14.8 us -> 0.06 us
    pallas_call x0 -> x5, Pallas kernels: none -> 124 us  [the longest x1 47.1 us: body(): pl.pallas_call(functools.partial(block_kernel, sizes), out_shape=(jax.Sha...]
    another operation x26 -> x0, other arithmetic: 109 us -> none  [the longest x4 47.1 us: body(): factors = jnp.linalg.cholesky(system)]
    scatter x16 -> x0, local copies, waits for them, and re-layouts: 42.5 us -> none  [advance_wide(): return state.at[:, 1:-1].set(updated)]
    psum x2 -> x0, blocking collectives: 33.4 us -> none  [the longest x1 17.1 us: body(): lax.psum((jnp.sum(misfit * misfit * weight), jnp.sum(live_mask * (spread...]
    gather x2 -> x0, local copies, waits for them, and re-layouts: 30.4 us -> none  [the longest x1 17.4 us: body(): obs_mean = jnp.take(realization_average, slot_cell_index)]
    all_gather x3 -> x0, waiting for transfers between devices: 27.7 us -> none  [the longest x1 27.7 us: body(): lax.all_gather(obs_anomaly, 'member', axis=0, tiled=True)]
    ppermute x6 -> x0, waiting for transfers between devices: 21.5 us -> none  [the longest x3 11.5 us: padded(): after = lax.ppermute(leading, axis, down)]
    min x32 -> x0, other arithmetic: 17.1 us -> none  [the longest x16 15.8 us: advance_wide(): fluxes = jnp.minimum(demand[:, :-1], supply[:, 1:])]
  transfers between devices with their start and end apart: 9 -> 0, of which waited for: 4 -> 0; matrix products, arithmetic and copies ran while one was open for 65% -> 0% of each run, Pallas kernels for 0% -> 0%
where the time goes in v1:
time: 130 us; the launch traced here: 129 us
  Pallas kernels  124 us (95%)
  local copies, waits for them, and re-layouts  4.67 us (4%)
    pallas_call x1, Pallas kernels, body(): pl.pallas_call(functools.partial(block_kernel, sizes), out_shape=(jax.Sha...  47.1 us
    pallas_call x1, Pallas kernels, body(): pl.pallas_call(functools.partial(scatter_kernel, sizes), out_shape=(jax.S...  24.5 us
    pallas_call x1, Pallas kernels, body(): pl.pallas_call(functools.partial(neighbour_kernel, sizes), out_shape=(jax...  18.9 us
    pallas_call x1, Pallas kernels, body(): pl.pallas_call(functools.partial(solve_kernel, sizes), out_shape=jax.Shap...  17.4 us
    pallas_call x1, Pallas kernels, body(): pl.pallas_call(functools.partial(return_kernel, sizes), out_shape=jax.Sha...  15.9 us

profile of v1, /device:TPU:0, one launch (start us, length us, event | category | flops | bytes accessed | tf_op | source)
XLA Modules:
  0.0 129.5 jit_solution(13437872611400140784)
XLA Ops:
  0.0 0.8 add_divide_fusion
  0.9 1.7 %stack.23.road = f32[8,8192]{1,0:T(8,128)} concatenate(f32[1,8192]{1,0:T(1,128)} %bitcast.7, f32[1,8192]{1,0:T(1,128)} %bitcast.8, f32[1,8192]{1,0:T(1,128)} %bitcast.9, f32[1,8192]{1,0:T(1,128)S(1)} %bitcast.10, f32[4,8192]{1,0:T(4,128)S(1)} %stack.22), dimensions={0} | concatenate | bytes 524288 | tf_op jit(solution)/shard_map/stack | solution.py:599
  2.6 24.5 %scatter.1 = (f32[128,2304]{1,0:T(8,128)}, f32[128,768]{1,0:T(8,128)}, f32[8,2304]{1,0:T(8,128)}) custom-call(f32[32,8192]{1,0:T(8,128)} %load.1, f32[32,3072]{1,0:T(8,128)} %noise.1, f32[8,8192]{1,0:T(8,128)} %stack.23.road), custom_call_target="tpu_custom_call" | custom-call | tf_op jit(solution)/shard_map/scatter/pallas_call | solution.py:601
  27.1 0.0 copy-start
  27.1 47.1 %block.1 = (f32[128,2048]{1,0:T(8,128)}, f32[8,2048]{1,0:T(8,128)}, f32[128,256]{1,0:T(8,128)}, f32[8,128]{1,0:T(8,128)}) custom-call(s32[4]{0:T(128)} %counts.1, f32[128,2304]{1,0:T(8,128)} %get-tuple-element.14.state, f32[128,768]{1,0:T(8,128)} %get-tuple-element.15.noise, f32[8,2304]{1,0:T(8,128)} %get-tuple-element.16.road, s32[1,3072]{1,0:T(1,128)} %bitcast.11, ...), custom_call_target="tpu_custom_call" | custom-call | tf_op jit(solution)/shard_map/block/pallas_call | solution.py:627
  74.2 0.0 copy-done
  74.2 0.2 convert_reduce_fusion
  74.4 0.1 copy.12
  74.5 0.6 reshape.20.select
  75.1 18.9 %neighbours.1 = (f32[128,256]{1,0:T(8,128)}, f32[8,128]{1,0:T(8,128)}) custom-call(f32[12]{0:T(128)} %reshape.20.select, f32[128,256]{1,0:T(8,128)} %get-tuple-element.17.products, f32[8,128]{1,0:T(8,128)} %get-tuple-element.18.parts), custom_call_target="tpu_custom_call" | custom-call | tf_op jit(solution)/shard_map/neighbours/pallas_call | solution.py:656
  93.9 17.4 %solve.1.result = f32[128,2048]{1,0:T(8,128)} custom-call(f32[128,256]{1,0:T(8,128)} %get-tuple-element.19.total, f32[8,128]{1,0:T(8,128)} %get-tuple-element.20.sums, f32[128,2048]{1,0:T(8,128)} %get-tuple-element.21.anomaly, f32[8,2048]{1,0:T(8,128)} %get-tuple-element.22.mean), custom_call_target="tpu_custom_call" | custom-call | tf_op jit(solution)/shard_map/solve/pallas_call | solution.py:684
  111.3 15.9 %give_back.1 = f32[32,8192]{1,0:T(8,128)} custom-call(f32[128,2048]{1,0:T(8,128)} %solve.1.result), custom_call_target="tpu_custom_call" | custom-call | tf_op jit(solution)/shard_map/give_back/pallas_call | solution.py:693
  127.2 2.3 %copy.14 = f32[32,8192]{1,0:T(8,128)} copy(f32[32,8192]{1,0:T(8,128)} %give_back.1) | data formatting | bytes 2097152
  (2 shorter events, 0.0 us)
Async XLA Ops:
  27.1 47.1 %copy-start = (s32[4,3]{1,0:T(4,128)S(1)}, s32[4,3]{1,0:T(4,128)}, u32[]{:S(2)}) copy-start(s32[4,3]{1,0:T(4,128)} %param.21) | copy-start | bytes 148

commit v2 on v1

--- a/solution.py
+++ b/solution.py
@@ -288,24 +288,28 @@
     for i in range(4):
         roads[i] = jnp.broadcast_to(road[i : i + 1, :], (8, width))
 
-    step_rows = 8
+    step_rows = 32
+
+    def wide(value):
+        return jnp.concatenate([value] * (step_rows // 8), axis=0)
 
     def group(g, total):
         here = pl.ds(pl.multiple_of(g * step_rows, step_rows), step_rows)
 
         def tick(_, now):
-            cap = roads[3]
-            demand = jnp.minimum(roads[0] * now, cap)
-            supply = jnp.minimum(cap, roads[1] * (roads[2] - now))
-            flux = jnp.minimum(demand, pltpu.roll(supply, width - 1, 1))
-            return now + pltpu.roll(flux, 1, 1) - flux
+            speed, wave, jam, cap = (wide(roads[i]) for i in range(4))
+            demand = jnp.minimum(speed * now, cap)
+            supply = jnp.minimum(cap, wave * (jam - now))
+            entering = jnp.minimum(pltpu.roll(demand, 1, 1), supply)
+            leaving = jnp.minimum(demand, pltpu.roll(supply, width - 1, 1))
+            return now + entering - leaving
 
         done = lax.fori_loop(0, HORIZON_TICKS, tick, state[here, :])
         inner = done[:, HALO : HALO + cells]
         forecast[here, :] = inner
-        return total + inner
-
-    total = lax.fori_loop(0, rows // step_rows, group, jnp.zeros((step_rows, cells), jnp.float32))
+        return total + sum(inner[8 * i : 8 * i + 8] for i in range(step_rows // 8))
+
+    total = lax.fori_loop(0, rows // step_rows, group, jnp.zeros((8, cells), jnp.float32))
     average = jnp.sum(total, axis=0, keepdims=True) / rows
     mean[...] = jnp.broadcast_to(average, mean.shape)
 

time: 130 us -> 104 us (0.80)
  Pallas kernels: 124 us -> 98.3 us
    pallas_call x1, Pallas kernels: 47.1 us -> 21.7 us  [body(): pl.pallas_call(functools.partial(block_kernel, sizes), out_shape=(jax.Sha...]
where the time goes in v2:
time: 104 us
  Pallas kernels  98.3 us (95%)
  local copies, waits for them, and re-layouts  4.67 us (4%)
    pallas_call x1, Pallas kernels, body(): pl.pallas_call(functools.partial(scatter_kernel, sizes), out_shape=(jax.S...  24.5 us
    pallas_call x1, Pallas kernels, body(): pl.pallas_call(functools.partial(block_kernel, sizes), out_shape=(jax.Sha...  21.7 us
    pallas_call x1, Pallas kernels, body(): pl.pallas_call(functools.partial(neighbour_kernel, sizes), out_shape=(jax...  18.9 us
    pallas_call x1, Pallas kernels, body(): pl.pallas_call(functools.partial(solve_kernel, sizes), out_shape=jax.Shap...  17.4 us
    pallas_call x1, Pallas kernels, body(): pl.pallas_call(functools.partial(return_kernel, sizes), out_shape=jax.Sha...  15.9 us
    unnamed x3, local copies, waits for them, and re-layouts  2.27 us

profile of v2, /device:TPU:0, one launch (start us, length us, event | category | flops | bytes accessed | tf_op | source)
XLA Modules:
  0.0 104.0 jit_solution(3146890027289337281)
XLA Ops:
  0.0 0.8 add_divide_fusion
  0.9 1.7 %stack.23.road = f32[8,8192]{1,0:T(8,128)} concatenate(f32[1,8192]{1,0:T(1,128)} %bitcast.7, f32[1,8192]{1,0:T(1,128)} %bitcast.8, f32[1,8192]{1,0:T(1,128)} %bitcast.9, f32[1,8192]{1,0:T(1,128)S(1)} %bitcast.10, f32[4,8192]{1,0:T(4,128)S(1)} %stack.22), dimensions={0} | concatenate | bytes 524288 | tf_op jit(solution)/shard_map/stack | solution.py:603
  2.6 24.5 %scatter.1 = (f32[128,2304]{1,0:T(8,128)}, f32[128,768]{1,0:T(8,128)}, f32[8,2304]{1,0:T(8,128)}) custom-call(f32[32,8192]{1,0:T(8,128)} %load.1, f32[32,3072]{1,0:T(8,128)} %noise.1, f32[8,8192]{1,0:T(8,128)} %stack.23.road), custom_call_target="tpu_custom_call" | custom-call | tf_op jit(solution)/shard_map/scatter/pallas_call | solution.py:605
  27.1 0.0 copy-start
  27.1 21.7 %block.1 = (f32[128,2048]{1,0:T(8,128)}, f32[8,2048]{1,0:T(8,128)}, f32[128,256]{1,0:T(8,128)}, f32[8,128]{1,0:T(8,128)}) custom-call(s32[4]{0:T(128)} %counts.1, f32[128,2304]{1,0:T(8,128)} %get-tuple-element.14.state, f32[128,768]{1,0:T(8,128)} %get-tuple-element.15.noise, f32[8,2304]{1,0:T(8,128)} %get-tuple-element.16.road, s32[1,3072]{1,0:T(1,128)} %bitcast.11, ...), custom_call_target="tpu_custom_call" | custom-call | tf_op jit(solution)/shard_map/block/pallas_call | solution.py:631
  48.8 0.0 copy-done
  48.8 0.2 convert_reduce_fusion
  49.0 0.1 copy.12
  49.1 0.6 reshape.20.select
  49.6 18.9 %neighbours.1 = (f32[128,256]{1,0:T(8,128)}, f32[8,128]{1,0:T(8,128)}) custom-call(f32[12]{0:T(128)} %reshape.20.select, f32[128,256]{1,0:T(8,128)} %get-tuple-element.17.products, f32[8,128]{1,0:T(8,128)} %get-tuple-element.18.parts), custom_call_target="tpu_custom_call" | custom-call | tf_op jit(solution)/shard_map/neighbours/pallas_call | solution.py:660
  68.5 17.4 %solve.1.result = f32[128,2048]{1,0:T(8,128)} custom-call(f32[128,256]{1,0:T(8,128)} %get-tuple-element.19.total, f32[8,128]{1,0:T(8,128)} %get-tuple-element.20.sums, f32[128,2048]{1,0:T(8,128)} %get-tuple-element.21.anomaly, f32[8,2048]{1,0:T(8,128)} %get-tuple-element.22.mean), custom_call_target="tpu_custom_call" | custom-call | tf_op jit(solution)/shard_map/solve/pallas_call | solution.py:688
  85.9 15.9 %give_back.1 = f32[32,8192]{1,0:T(8,128)} custom-call(f32[128,2048]{1,0:T(8,128)} %solve.1.result), custom_call_target="tpu_custom_call" | custom-call | tf_op jit(solution)/shard_map/give_back/pallas_call | solution.py:697
  101.8 2.3 %copy.14 = f32[32,8192]{1,0:T(8,128)} copy(f32[32,8192]{1,0:T(8,128)} %give_back.1) | data formatting | bytes 2097152
  (2 shorter events, 0.0 us)
Async XLA Ops:
  27.1 21.7 %copy-start = (s32[4,3]{1,0:T(4,128)S(1)}, s32[4,3]{1,0:T(4,128)}, u32[]{:S(2)}) copy-start(s32[4,3]{1,0:T(4,128)} %param.21) | copy-start | bytes 148
